TPU v7x, 32 devices: a whole 2x2x4 slice. The times are simulated.
32 devices in a mesh: mem: 8 (over z, y), hz: 4 (over x, core).
Axes of the slice: x: 2, y: 2, z: 4, core: 2. Of those that a mesh axis runs over, the one named last changes fastest.
Arguments:
- prior: float32 [8, 64, 32768], P('mem', None, 'hz'), may hold values from -6 to 6
- posterior: float32 [8, 64, 32768], P('mem', None, 'hz'), may hold values from -4 to 4
- control: float32 [64, 32768], P(None, 'hz'), may hold values from -6 to 6
- relax: float32 [64], replicated, may hold values from 0.5 to 0.95
- ocean: int32 [32768], P('hz'), may hold values 0 or 1
Outputs:
- analysis: float32 [8, 64, 32768], P('mem', None, 'hz')
All inputs are finite; a program needn't handle non-finite values. No bound on the sum of `ocean` on one device may be relied on, other than what follows from the above.
Results may differ from a plain program's by a relative error of at most 0.00002.
Values sent between devices are 32-bit elements; how exact they have to be, the bound alone decides.
A program may use at most 64 MiB of HBM per device.

v0:
```python
import jax
import jax.numpy as jnp
from jax import lax
from jax.sharding import PartitionSpec as P

eps = 1e-06


def inflation(relax, prior_spread, post_spread):
    return relax * (jnp.sqrt((prior_spread + eps) / (post_spread + eps)) - 1.0) + 1.0


def on_device(prior, posterior, control, relax, ocean):
    members = prior.shape[0] * lax.axis_size("mem")
    weights = ocean.astype(jnp.float32)
    prior_sq = jnp.sum(prior * prior * weights, axis=(0, 2))
    post_sq = jnp.sum(posterior * posterior * weights, axis=(0, 2))
    prior_total, post_total, prior_sq, post_sq = lax.psum(
        (jnp.sum(prior, axis=0), jnp.sum(posterior, axis=0), prior_sq, post_sq), "mem"
    )
    prior_mean = prior_total / members
    post_mean = post_total / members
    prior_local = prior_sq - members * jnp.sum(prior_mean * prior_mean * weights, axis=1)
    post_local = post_sq - members * jnp.sum(post_mean * post_mean * weights, axis=1)
    prior_spread, post_spread = lax.psum((prior_local, post_local), "hz")
    factor = inflation(relax, prior_spread, post_spread)
    return control + factor[None, :, None] * (posterior - post_mean)


def solution(mesh):
    return jax.shard_map(
        on_device,
        mesh=mesh,
        in_specs=(P("mem", None, "hz"), P("mem", None, "hz"), P(None, "hz"), P(), P("hz")),
        out_specs=P("mem", None, "hz"),
        check_vma=False,
    )
```

profile of v0, /device:TPU:0, one launch (start us, length us, event | category | flops | bytes accessed | tf_op | source)
XLA Modules:
  0.0 194.0 jit_solution(6217947592107663608)
XLA Ops:
  6.5 0.8 convert_element_type.3
  7.3 2.7 %multiply_reduce_fusion.3 = (f32[64]{0:T(128)S(1)}, f32[64]{0:T(128)S(1)}) fusion(f32[1,64,8192]{2,1,0:T(8,128)} %param.5, f32[8192]{0:T(1024)S(1)} %convert_element_type.3, f32[1,64,8192]{2,1,0:T(8,128)} %param.6), kind=kLoop, calls=%fused_computation.6 | loop fusion | flops 3145600 | bytes 4227584 | tf_op jit(solution)/shard_map/reduce_sum | solution.py:16
  10.0 0.0 all-reduce.5.cloned.1.call-start
  10.1 0.7 all-reduce.5.cloned.1.call-update
  10.8 23.9 %all-reduce = (f32[64]{0:T(128)S(1)}, f32[64]{0:T(128)S(1)}) all-reduce(f32[64]{0:T(128)S(1)} %get-tuple-element.8, f32[64]{0:T(128)S(1)} %get-tuple-element.7), channel_id=1, replica_groups=mesh['mem'=8,'hz'=4] {'mem'}, use_global_device_ids=true, to_apply=%region_6.0 | all-reduce | flops 128 | bytes 1024 | tf_op jit(solution)/shard_map/psum | solution.py:18
  34.7 139.1 %all-reduce.5.cloned.1.call-done = (f32[64,8192]{1,0:T(8,128)}, f32[64,8192]{1,0:T(8,128)}) async-done(((f32[64,8192]{1,0:T(8,128)}, f32[64,8192]{1,0:T(8,128)}), (f32[64,8192]{1,0:T(8,128)}, f32[64,8192]{1,0:T(8,128)})) %all-reduce.5.cloned.1.call-update) | async-done | bytes 4194320 | tf_op jit(solution)/shard_map/psum | solution.py:18
  173.8 0.0 copy-start.1
  173.8 0.0 copy-start
  173.8 3.0 %multiply_reduce_fusion.2 = (f32[64]{0:T(128)S(1)}, f32[64]{0:T(128)S(1)}) fusion(f32[64,8192]{1,0:T(8,128)} %get-tuple-element.12, f32[8192]{0:T(1024)S(1)} %convert_element_type.3, f32[64,8192]{1,0:T(8,128)} %get-tuple-element.11), kind=kLoop, calls=%fused_computation.5 | loop fusion | flops 4194176 | bytes 4227584 | tf_op jit(solution)/shard_map/reduce_sum | solution.py:23
  176.8 6.4 %all-reduce.2 = (f32[64]{0:T(128)S(1)}, f32[64]{0:T(128)S(1)}) all-reduce(f32[64]{0:T(128)S(1)} %get-tuple-element.15, f32[64]{0:T(128)S(1)} %get-tuple-element.16), channel_id=1, replica_groups=mesh['mem'=8,'hz'=4] {'hz'}, use_global_device_ids=true, to_apply=%region_9.0 | all-reduce | flops 128 | bytes 1024 | tf_op jit(solution)/shard_map/psum | solution.py:25
  183.2 0.0 copy-done.1
  183.2 0.0 copy-done
  183.3 3.9 %fusion.1 = f32[1,64,8192]{2,1,0:T(8,128)} fusion(f32[1,64,8192]{2,1,0:T(8,128)S(1)} %copy-done, f32[64,8192]{1,0:T(8,128)} %param.7, f32[64,8192]{1,0:T(8,128)} %get-tuple-element.11, f32[64]{0:T(128)S(1)} %multiply_add_fusion), kind=kLoop, calls=%fused_computation.2 | loop fusion | flops 2097152 | bytes 8388864 | tf_op jit(solution)/shard_map/add | solution.py:27
  (2 shorter events, 0.0 us)
Async XLA Ops:
  10.0 163.8 %all-reduce.5.cloned.1.call-start = ((), (), s32[]{:S(2)}) async-start(), calls=%async_computation | async-start | bytes 8388608 | tf_op jit(solution)/shard_map/psum | solution.py:18
  173.8 9.4 %copy-start.1 = (f32[64]{0:T(128)S(1)}, f32[64]{0:T(128)}, u32[]{:S(2)}) copy-start(f32[64]{0:T(128)} %param.8) | copy-start | bytes 772
  173.8 9.4 %copy-start = (f32[1,64,8192]{2,1,0:T(8,128)S(1)}, f32[1,64,8192]{2,1,0:T(8,128)}, u32[]{:S(2)}) copy-start(f32[1,64,8192]{2,1,0:T(8,128)} %param.6) | copy-start | bytes 6291460
Sparse Core Ops, SparseCore 0:
  14.6 159.1 all-reduce.4
where the time goes:
time: 194 us
  waiting for transfers between devices  140 us (72%)
  blocking collectives  30.3 us (16%)
  between operations  13.4 us (7%)
  other arithmetic  10.4 us (5%)
    psum x1, waiting for transfers between devices, on_device(): lax.psum((jnp.sum(prior, axis=0), jnp.sum(posterior, axis=0), prior_sq, p...  139 us
    psum x1, blocking collectives, on_device(): lax.psum((jnp.sum(prior, axis=0), jnp.sum(posterior, axis=0), prior_sq, p...  23.9 us
    psum x1, blocking collectives, on_device(): prior_spread, post_spread = lax.psum((prior_local, post_local), 'hz')  6.4 us
    add x1, other arithmetic, on_device(): return control + factor[None, :, None] * (posterior - post_mean)  3.88 us
  transfers between devices with their start and end apart: 1, of which 1 were waited for; matrix products, arithmetic and copies ran while one was open for 0% of the time, Pallas kernels for 0%

commit v1 on v0

v1 whole, which is shorter than its diff:
```python
import functools

import jax
import jax.numpy as jnp
from jax import lax
from jax.experimental import pallas as pl
from jax.experimental.pallas import tpu as pltpu
from jax.sharding import PartitionSpec as P

eps = 1e-06
SUB = 8
LANE = 128
LAG = 2
MESH = pl.DeviceIdType.MESH
POST, PRIOR = 0, 1


def kernel(members, blocks, prior_hbm, post_hbm, control_hbm, relax_ref, ocean_ref, out_hbm,
           x, control, weights, total, out, y_in, pair, a_in, b_in, b_sum, b_swap, b_swap_prior, spread, part1, part2, zero,
           load_sem, control_sem, out_sem, y_send, y_recv, a_send, a_recv, b_send, b_recv, s_send, s_recv, p_send, p_recv,
           ga_send, ga_recv, gy_send, gy_recv, gb_send, gb_recv, h_send, h_recv, m_send, m_recv):
    levels, columns = control.shape
    half = columns // 2
    nblocks = levels // SUB
    quarter = nblocks // 4
    depth = members // 2
    m = lax.axis_index("mem")
    hz = lax.axis_index("hz")
    z = lax.div(m, 2)
    y = lax.rem(m, 2)
    other = 1 - y

    def device(zz, yy):
        return {"mem": zz * 2 + yy, "hz": hz}

    def rows(block):
        return pl.ds(pl.multiple_of(block * SUB, SUB), SUB)

    def cols(h):
        return pl.ds(pl.multiple_of(h * half, LANE), half)

    fields = (post_hbm, prior_hbm)

    def load(field, block):
        at = pl.ds(block * SUB, SUB)
        return pltpu.make_async_copy(fields[field].at[0, at], x.at[field, at], load_sem.at[field, block])

    order = []
    for i in range(2 * quarter):
        order += [i, 2 * quarter + i]
    for field in (POST, PRIOR):
        for block in order:
            load(field, block).start()
    control_load = pltpu.make_async_copy(control_hbm, control, control_sem)
    control_load.start()

    barrier = pltpu.get_barrier_semaphore()
    for i in range(1, members):
        pl.semaphore_signal(barrier, inc=1, device_id={"mem": lax.rem(m + i, members), "hz": hz}, device_id_type=MESH)
    for i in range(1, blocks):
        pl.semaphore_signal(barrier, inc=1, device_id={"mem": m, "hz": lax.rem(hz + i, blocks)}, device_id_type=MESH)
    weights[...] = jnp.broadcast_to(ocean_ref[...].astype(jnp.float32), (SUB, columns))
    spread[...] = jnp.zeros_like(spread)
    pl.semaphore_wait(barrier, members - 1 + blocks - 1)

    pending = []

    def send(src, dst, send_sem, recv_sem, to, cond=None):
        copy = pltpu.make_async_remote_copy(src_ref=src, dst_ref=dst, send_sem=send_sem, recv_sem=recv_sem,
                                            device_id=to, device_id_type=MESH)
        if cond is None:
            copy.start()
        else:
            pl.when(cond)(copy.start)
        pending.append((cond, copy))

    def arrive(dst, send_sem, recv_sem):
        pltpu.make_async_remote_copy(src_ref=dst, dst_ref=dst, send_sem=send_sem, recv_sem=recv_sem,
                                     device_id=device(z, other), device_id_type=MESH).wait_recv()

    def merge(own, n_own, came, n_came, dst, field, block, h, scale=None):
        n_own = jnp.float32(n_own)
        n_came = jnp.float32(n_came) if isinstance(n_came, int) else n_came.astype(jnp.float32)
        w = weights.at[:, cols(h)]
        acc = jnp.zeros((SUB, LANE), jnp.float32)
        for j in range(half // LANE):
            at = slice(j * LANE, (j + 1) * LANE)
            a, b = own[:, at], came[:, at]
            d = b * n_own - a * n_came
            acc += d * d * w[:, at]
            if dst is not None:
                dst[:, at] = a + b
        acc = acc / jnp.full((SUB, LANE), n_own * n_came * (n_own + n_came), jnp.float32)
        if scale is not None:
            acc = acc * scale
        spread[field, block] += acc

    up_near = 2 * z < depth
    near = jnp.where(up_near, 0, 1)
    far = 1 - near

    def place(d):
        at = jnp.where(d == 0, z, depth - 1 - z)
        return at, z + 1 - 2 * d, z - 1 + 2 * d

    def first(field):
        for i in range(2 * quarter):
            load(field, i).wait()
            send(x.at[field, pl.ds(i * SUB, SUB), cols(other)], y_in.at[field, i], y_send.at[field, i], y_recv.at[field, i],
                 device(z, other))
            load(field, 2 * quarter + i).wait()
        for k in range(quarter):
            for h in range(2):
                for d in (0, 1):
                    at, nxt, _ = place(d)
                    i = d * quarter + k
                    send(x.at[field, pl.ds((2 * quarter + i) * SUB, SUB), pl.ds(h * half, half)], b_in.at[field, i, h],
                         b_send.at[field, i, h], b_recv.at[field, i, h], device(nxt, y), (at == 0) & (at < depth - 1))

    def pair_step(field, i):
        arrive(y_in.at[field, i], y_send.at[field, i], y_recv.at[field, i])
        merge(x.at[field, pl.ds(i * SUB, SUB), cols(y)], 1, y_in.at[field, i], 1, pair.at[field, i], field, i, y)

    def a_step(field, d, k):
        at, nxt, back = place(d)
        i = d * quarter + k
        mine = pair.at[field, i]

        @pl.when(at > 0)
        def _():
            arrive(a_in.at[field, i], a_send.at[field, i], a_recv.at[field, i])
            merge(mine, 2, a_in.at[field, i], 2 * at, mine, field, i, y)

        send(mine, a_in.at[field, i], a_send.at[field, i], a_recv.at[field, i], device(nxt, y), at < depth - 1)
        if field == POST:
            last = at == depth - 1
            spot = total.at[rows(i), cols(y)]

            @pl.when(last)
            def _():
                spot[...] = mine[...]

            send(mine, spot, ga_send.at[i], ga_recv.at[i], device(back, y), last & (at > 0))
            send(mine, spot, gy_send.at[i], gy_recv.at[i], device(z, other), last)

    def b_step(field, d, k, h):
        at, nxt, _ = place(d)
        i = d * quarter + k
        block = 2 * quarter + i
        own = x.at[field, rows(block), cols(h)]
        mine = b_sum.at[field, i, h]

        @pl.when(at > 0)
        def _():
            arrive(b_in.at[field, i, h], b_send.at[field, i, h], b_recv.at[field, i, h])
            merge(own, 1, b_in.at[field, i, h], at, mine, field, block, h)

        last = at == depth - 1
        send(mine, b_in.at[field, i, h], b_send.at[field, i, h], b_recv.at[field, i, h], device(nxt, y), (at > 0) & ~last)
        if field == POST:
            send(mine, b_swap.at[i, h], s_send.at[i, h], s_recv.at[i, h], device(z, other), last)
        else:
            send(mine, b_swap_prior.at[i], p_send.at[i], p_recv.at[i], device(z, other), last & (other == h))

    def swap_step(d, k, h):
        at, _, back = place(d)
        i = d * quarter + k
        block = 2 * quarter + i
        last = at == depth - 1
        spot = total.at[rows(block), pl.ds(h * half, half)]

        @pl.when(last)
        def _():
            arrive(b_swap.at[i, h], s_send.at[i, h], s_recv.at[i, h])
            merge(b_sum.at[POST, i, h], depth, b_swap.at[i, h], depth, spot, POST, block, h, jnp.where(y == h, 1.0, 0.0))

        send(spot, spot, gb_send.at[i, h], gb_recv.at[i, h], device(back, y), last & (at > 0))

    def swap_prior(d, k):
        at, _, _ = place(d)
        i = d * quarter + k

        @pl.when(at == depth - 1)
        def _():
            arrive(b_swap_prior.at[i], p_send.at[i], p_recv.at[i])
            merge(b_sum.at[PRIOR, i, y], depth, b_swap_prior.at[i], depth, None, PRIOR, 2 * quarter + i, y)

    def a_relay(d, k):
        at, _, back = place(d)
        i = d * quarter + k
        spot = total.at[rows(i), cols(y)]
        below = at < depth - 1

        @pl.when(below)
        def _():
            arrive(spot, ga_send.at[i], ga_recv.at[i])

        send(spot, spot, ga_send.at[i], ga_recv.at[i], device(back, y), below & (at > 0))
        send(spot, spot, gy_send.at[i], gy_recv.at[i], device(z, other), below)

    def b_relay(d, k, h):
        at, _, back = place(d)
        i = d * quarter + k
        spot = total.at[rows(2 * quarter + i), pl.ds(h * half, half)]
        below = at < depth - 1

        @pl.when(below)
        def _():
            arrive(spot, gb_send.at[i, h], gb_recv.at[i, h])

        send(spot, spot, gb_send.at[i, h], gb_recv.at[i, h], device(back, y), below & (at > 0))

    first(POST)
    first(PRIOR)

    def chain(field):
        steps = []
        for k in range(quarter):
            for h in range(2):
                steps.append(functools.partial(lambda k, h, d: b_step(field, d, k, h), k, h))
        for k in range(quarter):
            steps.append(functools.partial(lambda k, d: a_step(field, d, k), k))
        return steps

    post_steps, prior_steps = chain(POST), chain(PRIOR)
    nb = 2 * quarter
    pairs = [(POST, i) for i in range(2 * quarter)] + [(PRIOR, i) for i in range(2 * quarter)]
    swaps = [functools.partial(lambda k, h, d: swap_step(d, k, h), k, h) for k in range(quarter) for h in range(2)]
    steps = post_steps + prior_steps
    n = len(steps)
    done_pairs = 0
    for s in range(n + LAG):
        if done_pairs < len(pairs):
            pair_step(*pairs[done_pairs])
            done_pairs += 1
        if s < n:
            steps[s](near)
        if s >= LAG:
            steps[s - LAG](far)
        t = s - LAG - nb
        if 0 <= t < len(swaps):
            swaps[t](0)
            swaps[t](1)
    for k in range(quarter):
        swap_prior(0, k)
        swap_prior(1, k)

    lane = lax.broadcasted_iota(jnp.int32, (SUB, LANE), 1)
    for field in (POST, PRIOR):
        packed = jnp.zeros((SUB, LANE), jnp.float32)
        for block in range(nblocks):
            packed = jnp.where(lane == block, jnp.sum(spread[field, block], axis=1, keepdims=True), packed)
        part1[hz, field] = packed
    for i in range(1, blocks):
        send(part1.at[hz], part1.at[hz], h_send.at[i], h_recv.at[hz], {"mem": m, "hz": lax.rem(hz + i, blocks)})

    units = [(None, k) for k in range(quarter)] + [(h, k) for k in range(quarter) for h in range(2)]

    def relay(d, h, k):
        if h is None:
            a_relay(d, k)
        else:
            b_relay(d, k, h)

    events = []
    for s in range(len(units) + 1):
        if s < len(units):
            events.append((far, *units[s]))
        if s >= 1:
            events.append((near, *units[s - 1]))
    cut1, cut2 = len(events) // 3, 2 * len(events) // 3
    for event in events[:cut1]:
        relay(*event)
    for i in range(1, blocks):
        src = lax.rem(hz + i, blocks)
        arrive(part1.at[src], h_send.at[i], h_recv.at[src])
    for field in (POST, PRIOR):
        v = part1[0, field]
        for i in range(1, blocks):
            v = v + part1[i, field]
        part2[m, field] = v
    for i in range(1, members):
        send(part2.at[m], part2.at[m], m_send.at[i], m_recv.at[m], {"mem": lax.rem(m + i, members), "hz": hz})
    for event in events[cut1:cut2]:
        relay(*event)
    for i in range(1, members):
        src = lax.rem(m + i, members)
        arrive(part2.at[src], m_send.at[i], m_recv.at[src])
    spreads = []
    for field in (POST, PRIOR):
        v = part2[0, field]
        for i in range(1, members):
            v = v + part2[i, field]
        spreads.append(v)
    sub = lax.broadcasted_iota(jnp.int32, (SUB, LANE), 0)
    relax = jnp.zeros((SUB, LANE), jnp.float32)
    for level in range(levels):
        relax = jnp.where((sub == level % SUB) & (lane == level // SUB), relax_ref[level], relax)
    factor = relax * (jnp.sqrt((spreads[PRIOR] + eps) / (spreads[POST] + eps)) - 1.0) + 1.0
    for block in range(nblocks):
        zero[block] = jnp.broadcast_to(
            jnp.sum(jnp.where(lane == block, factor, 0.0), axis=1, keepdims=True), (SUB, LANE))
    control_load.wait()

    outs = []

    def finish(block, h):
        f = zero[block]
        c, p, t, o = (r.at[rows(block), cols(h)] for r in (control, x.at[POST], total, out))
        for j in range(half // LANE):
            at = slice(j * LANE, (j + 1) * LANE)
            o[:, at] = c[:, at] + f * (p[:, at] - t[:, at] / members)
        copy = pltpu.make_async_copy(o, out_hbm.at[0, rows(block), cols(h)], out_sem.at[block, h])
        copy.start()
        outs.append(copy)

    for i, (d, h, k) in enumerate(events):
        if i >= cut2:
            relay(d, h, k)
        if h is None:
            finish(d * quarter + k, y)
        else:
            finish(2 * quarter + d * quarter + k, h)
    for k in range(quarter):
        for d in (near, far):
            i = d * quarter + k
            arrive(total.at[rows(i), cols(other)], gy_send.at[i], gy_recv.at[i])
            finish(i, other)
    for cond, copy in pending:
        if cond is None:
            copy.wait_send()
        else:
            pl.when(cond)(copy.wait_send)
    for copy in outs:
        copy.wait()


def solution(mesh):
    members, blocks = mesh.shape["mem"], mesh.shape["hz"]

    def on_device(prior, posterior, control, relax, ocean):
        levels, columns = control.shape
        half, nblocks = columns // 2, levels // SUB
        a, q = nblocks // 2, nblocks // 4
        vmem = lambda *shape: pltpu.VMEM(shape, jnp.float32)
        dma = lambda *shape: pltpu.SemaphoreType.DMA(shape)
        hbm = pl.BlockSpec(memory_space=pl.ANY)
        return pl.pallas_call(
            functools.partial(kernel, members, blocks),
            out_shape=jax.ShapeDtypeStruct(posterior.shape, jnp.float32),
            in_specs=[hbm, hbm, hbm, pl.BlockSpec(memory_space=pltpu.SMEM), pl.BlockSpec(memory_space=pltpu.VMEM)],
            out_specs=hbm,
            scratch_shapes=[
                vmem(2, levels, columns), vmem(levels, columns), vmem(SUB, columns), vmem(levels, columns),
                vmem(levels, columns), vmem(2, a, SUB, half), vmem(2, a, SUB, half), vmem(2, a, SUB, half),
                vmem(2, a, 2, SUB, half), vmem(2, a, 2, SUB, half), vmem(a, 2, SUB, half), vmem(a, SUB, half),
                vmem(2, nblocks, SUB, LANE), vmem(blocks, 2, SUB, LANE), vmem(members, 2, SUB, LANE),
                vmem(nblocks, SUB, LANE),
                dma(2, nblocks), pltpu.SemaphoreType.DMA, dma(nblocks, 2),
                dma(2, a), dma(2, a), dma(2, a), dma(2, a), dma(2, a, 2), dma(2, a, 2), dma(a, 2), dma(a, 2), dma(a), dma(a),
                dma(a), dma(a), dma(a), dma(a), dma(a, 2), dma(a, 2), dma(blocks), dma(blocks), dma(members), dma(members),
            ],
            compiler_params=pltpu.CompilerParams(
                collective_id=0, has_side_effects=True, vmem_limit_bytes=60 * 2**20
            ),
        )(prior, posterior, control, relax, ocean.reshape(1, columns))

    return jax.shard_map(
        on_device,
        mesh=mesh,
        in_specs=(P("mem", None, "hz"), P("mem", None, "hz"), P(None, "hz"), P(), P("hz")),
        out_specs=P("mem", None, "hz"),
        check_vma=False,
    )
```

time: 194 us -> 108 us (0.56)
  waiting for transfers between devices: 140 us -> 0 us
  Pallas kernels: 0 us -> 105 us
  blocking collectives: 30.3 us -> 0 us
  between operations: 13.4 us -> 0.01 us
  other arithmetic: 10.4 us -> 0 us
  local copies, waits for them, and re-layouts: 0.01 us -> 3.06 us
    psum x1 -> x0, waiting for transfers between devices: 139 us -> none  [on_device(): lax.psum((jnp.sum(prior, axis=0), jnp.sum(posterior, axis=0), prior_sq, p...]
    pallas_call x0 -> x1, Pallas kernels: none -> 105 us  [on_device(): pl.pallas_call(functools.partial(kernel, members, blocks), out_shape=jax....]
    psum x2 -> x0, blocking collectives: 30.3 us -> none  [the longest x1 23.9 us: on_device(): lax.psum((jnp.sum(prior, axis=0), jnp.sum(posterior, axis=0), prior_sq, p...]
    reduce_sum x2 -> x0, other arithmetic: 5.74 us -> none  [the longest x1 3.01 us: on_device(): jnp.sum(prior_mean * prior_mean * weights, axis=1)]
    add x2 -> x0, other arithmetic: 3.89 us -> none  [the longest x1 3.88 us: on_device(): return control + factor[None, :, None] * (posterior - post_mean)]
    unnamed x4 -> x1, local copies, waits for them, and re-layouts: 0.01 us -> 3.06 us
  transfers between devices with their start and end apart: 1 -> 0, of which waited for: 1 -> 0; matrix products, arithmetic and copies ran while one was open for 0% -> 0% of each run, Pallas kernels for 0% -> 0%
where the time goes in v1:
time: 108 us
  Pallas kernels  105 us (97%)
  local copies, waits for them, and re-layouts  3.06 us (3%)
    pallas_call x1, Pallas kernels, on_device(): pl.pallas_call(functools.partial(kernel, members, blocks), out_shape=jax....  105 us
    unnamed x1, local copies, waits for them, and re-layouts  3.06 us

profile of v1, /device:TPU:0, one launch (start us, length us, event | category | flops | bytes accessed | tf_op | source)
XLA Modules:
  0.0 108.0 jit_solution(2731238610932245401)
XLA Ops:
  0.0 105.0 %shard_map.55 = f32[1,64,8192]{2,1,0:T(8,128)} custom-call(f32[1,64,8192]{2,1,0:T(8,128)} %prior_hbm.1, f32[1,64,8192]{2,1,0:T(8,128)} %post_hbm.1, f32[64,8192]{1,0:T(8,128)} %control_hbm.1, f32[64]{0:T(128)} %relax_ref.1, s32[1,8192]{1,0:T(1,128)} %bitcast.1), custom_call_target="tpu_custom_call" | custom-call | tf_op jit(solution)/shard_map/pallas_call | solution.py:348
  105.0 3.1 %copy.7 = f32[1,64,8192]{2,1,0:T(8,128)} copy(f32[1,64,8192]{2,1,0:T(8,128)} %shard_map.55) | data formatting | bytes 4194304

commit v2 on v1

--- a/solution.py
+++ b/solution.py
@@ -104,22 +104,29 @@
         return at, z + 1 - 2 * d, z - 1 + 2 * d
 
     def first(field):
-        for i in range(2 * quarter):
-            load(field, i).wait()
-            send(x.at[field, pl.ds(i * SUB, SUB), cols(other)], y_in.at[field, i], y_send.at[field, i], y_recv.at[field, i],
-                 device(z, other))
-            load(field, 2 * quarter + i).wait()
+        for block in order:
+            load(field, block).wait()
+        for d in (near, far):
+            for k in range(quarter):
+                i = d * quarter + k
+                send(x.at[field, rows(i), cols(other)], y_in.at[field, i], y_send.at[field, i], y_recv.at[field, i],
+                     device(z, other))
+
+    def start_b(field):
+        at, nxt, _ = place(near)
         for k in range(quarter):
             for h in range(2):
-                for d in (0, 1):
-                    at, nxt, _ = place(d)
-                    i = d * quarter + k
-                    send(x.at[field, pl.ds((2 * quarter + i) * SUB, SUB), pl.ds(h * half, half)], b_in.at[field, i, h],
-                         b_send.at[field, i, h], b_recv.at[field, i, h], device(nxt, y), (at == 0) & (at < depth - 1))
-
-    def pair_step(field, i):
+                i = near * quarter + k
+                send(x.at[field, rows(2 * quarter + i), pl.ds(h * half, half)], b_in.at[field, i, h],
+                     b_send.at[field, i, h], b_recv.at[field, i, h], device(nxt, y), (at == 0) & (at < depth - 1))
+
+    def pair_step(field, d, k):
+        at, nxt, _ = place(d)
+        i = d * quarter + k
+        mine = pair.at[field, i]
         arrive(y_in.at[field, i], y_send.at[field, i], y_recv.at[field, i])
-        merge(x.at[field, pl.ds(i * SUB, SUB), cols(y)], 1, y_in.at[field, i], 1, pair.at[field, i], field, i, y)
+        merge(x.at[field, rows(i), cols(y)], 1, y_in.at[field, i], 1, mine, field, i, y)
+        send(mine, a_in.at[field, i], a_send.at[field, i], a_recv.at[field, i], device(nxt, y), (at == 0) & (at < depth - 1))
 
     def a_step(field, d, k):
         at, nxt, back = place(d)
@@ -131,7 +138,7 @@
             arrive(a_in.at[field, i], a_send.at[field, i], a_recv.at[field, i])
             merge(mine, 2, a_in.at[field, i], 2 * at, mine, field, i, y)
 
-        send(mine, a_in.at[field, i], a_send.at[field, i], a_recv.at[field, i], device(nxt, y), at < depth - 1)
+        send(mine, a_in.at[field, i], a_send.at[field, i], a_recv.at[field, i], device(nxt, y), (at > 0) & (at < depth - 1))
         if field == POST:
             last = at == depth - 1
             spot = total.at[rows(i), cols(y)]
@@ -211,6 +218,7 @@
         send(spot, spot, gb_send.at[i, h], gb_recv.at[i, h], device(back, y), below & (at > 0))
 
     first(POST)
+    start_b(POST)
     first(PRIOR)
 
     def chain(field):
@@ -224,7 +232,7 @@
 
     post_steps, prior_steps = chain(POST), chain(PRIOR)
     nb = 2 * quarter
-    pairs = [(POST, i) for i in range(2 * quarter)] + [(PRIOR, i) for i in range(2 * quarter)]
+    pairs = [(field, d, k) for field in (POST, PRIOR) for d in (near, far) for k in range(quarter)]
     swaps = [functools.partial(lambda k, h, d: swap_step(d, k, h), k, h) for k in range(quarter) for h in range(2)]
     steps = post_steps + prior_steps
     n = len(steps)
@@ -233,11 +241,13 @@
         if done_pairs < len(pairs):
             pair_step(*pairs[done_pairs])
             done_pairs += 1
+            if done_pairs == quarter:
+                start_b(PRIOR)
         if s < n:
             steps[s](near)
         if s >= LAG:
             steps[s - LAG](far)
-        t = s - LAG - nb
+        t = s - LAG - nb - 1
         if 0 <= t < len(swaps):
             swaps[t](0)
             swaps[t](1)

time: 108 us -> 76.7 us (0.71)
  Pallas kernels: 105 us -> 73.4 us
    pallas_call x1, Pallas kernels: 105 us -> 73.4 us  [on_device(): pl.pallas_call(functools.partial(kernel, members, blocks), out_shape=jax....]
where the time goes in v2:
time: 76.7 us; the launch traced here: 76.5 us
  Pallas kernels  73.4 us (96%)
  local copies, waits for them, and re-layouts  3.06 us (4%)
    pallas_call x1, Pallas kernels, on_device(): pl.pallas_call(functools.partial(kernel, members, blocks), out_shape=jax....  73.4 us
    unnamed x1, local copies, waits for them, and re-layouts  3.06 us

profile of v2, /device:TPU:0, one launch (start us, length us, event | category | flops | bytes accessed | tf_op | source)
XLA Modules:
  0.0 76.5 jit_solution(2920251808228188117)
XLA Ops:
  0.0 73.4 %shard_map.55 = f32[1,64,8192]{2,1,0:T(8,128)} custom-call(f32[1,64,8192]{2,1,0:T(8,128)} %prior_hbm.1, f32[1,64,8192]{2,1,0:T(8,128)} %post_hbm.1, f32[64,8192]{1,0:T(8,128)} %control_hbm.1, f32[64]{0:T(128)} %relax_ref.1, s32[1,8192]{1,0:T(1,128)} %bitcast.1), custom_call_target="tpu_custom_call" | custom-call | tf_op jit(solution)/shard_map/pallas_call | solution.py:358
  73.4 3.1 %copy.7 = f32[1,64,8192]{2,1,0:T(8,128)} copy(f32[1,64,8192]{2,1,0:T(8,128)} %shard_map.55) | data formatting | bytes 4194304

commit v3 on v2

--- a/solution.py
+++ b/solution.py
@@ -236,6 +236,21 @@
     swaps = [functools.partial(lambda k, h, d: swap_step(d, k, h), k, h) for k in range(quarter) for h in range(2)]
     steps = post_steps + prior_steps
     n = len(steps)
+    units = [(None, k) for k in range(quarter)] + [(h, k) for k in range(quarter) for h in range(2)]
+
+    def relay(d, h, k):
+        if h is None:
+            a_relay(d, k)
+        else:
+            b_relay(d, k, h)
+
+    events = []
+    for u in range(len(units) + 1):
+        if u < len(units):
+            events.append((far, *units[u]))
+        if u >= 1:
+            events.append((near, *units[u - 1]))
+    cut1, cut2 = len(events) // 3, 2 * len(events) // 3
     done_pairs = 0
     for s in range(n + LAG):
         if done_pairs < len(pairs):
@@ -251,6 +266,8 @@
         if 0 <= t < len(swaps):
             swaps[t](0)
             swaps[t](1)
+        if s == n + LAG - 2:
+            relay(*events[0])
     for k in range(quarter):
         swap_prior(0, k)
         swap_prior(1, k)
@@ -264,22 +281,7 @@
     for i in range(1, blocks):
         send(part1.at[hz], part1.at[hz], h_send.at[i], h_recv.at[hz], {"mem": m, "hz": lax.rem(hz + i, blocks)})
 
-    units = [(None, k) for k in range(quarter)] + [(h, k) for k in range(quarter) for h in range(2)]
-
-    def relay(d, h, k):
-        if h is None:
-            a_relay(d, k)
-        else:
-            b_relay(d, k, h)
-
-    events = []
-    for s in range(len(units) + 1):
-        if s < len(units):
-            events.append((far, *units[s]))
-        if s >= 1:
-            events.append((near, *units[s - 1]))
-    cut1, cut2 = len(events) // 3, 2 * len(events) // 3
-    for event in events[:cut1]:
+    for event in events[1:cut1]:
         relay(*event)
     for i in range(1, blocks):
         src = lax.rem(hz + i, blocks)

time: 76.7 us -> 76.4 us (level)
  no operation moved by 1% of the time
where the time goes in v3:
time: 76.4 us; the launch traced here: 76.2 us
  Pallas kernels  73.1 us (96%)
  local copies, waits for them, and re-layouts  3.06 us (4%)
    pallas_call x1, Pallas kernels, on_device(): pl.pallas_call(functools.partial(kernel, members, blocks), out_shape=jax....  73.1 us
    unnamed x1, local copies, waits for them, and re-layouts  3.06 us

profile of v3, /device:TPU:0, one launch (start us, length us, event | category | flops | bytes accessed | tf_op | source)
XLA Modules:
  0.0 76.2 jit_solution(3117724771981400080)
XLA Ops:
  0.0 73.1 %shard_map.55 = f32[1,64,8192]{2,1,0:T(8,128)} custom-call(f32[1,64,8192]{2,1,0:T(8,128)} %prior_hbm.1, f32[1,64,8192]{2,1,0:T(8,128)} %post_hbm.1, f32[64,8192]{1,0:T(8,128)} %control_hbm.1, f32[64]{0:T(128)} %relax_ref.1, s32[1,8192]{1,0:T(1,128)} %bitcast.1), custom_call_target="tpu_custom_call" | custom-call | tf_op jit(solution)/shard_map/pallas_call | solution.py:360
  73.1 3.1 %copy.7 = f32[1,64,8192]{2,1,0:T(8,128)} copy(f32[1,64,8192]{2,1,0:T(8,128)} %shard_map.55) | data formatting | bytes 4194304
